TPU v7x, 256 devices: a whole 4x4x8 slice. The times are simulated.
256 devices in a mesh: dp: 8 (over x, core), expert: 32 (over z, y).
Axes of the slice: x: 4, y: 4, z: 8, core: 2. Of those that a mesh axis runs over, the one named last changes fastest.
Arguments:
- tokens: bfloat16 [2048, 6144], P('dp', 'expert'), may hold values from -6 to 6
- cotangent: bfloat16 [2048, 6144], P('dp', 'expert'), may hold values from -6 to 6
- expert_choice: int32 [2048, 2], P('dp'), may hold values from 0 to 7, all different within a row; in each aligned block of 256 rows (0 to 255, 256 to 511, ...) at most 80 rows name the same one
- gate_values: bfloat16 [2048, 2], P('dp'), may hold values from 0.099609375 to 1
- gate_weight: bfloat16 [8, 6144, 8192], P('dp', None, 'expert'), may hold values from -0.078125 to 0.078125
- up_weight: bfloat16 [8, 6144, 8192], P('dp', None, 'expert'), may hold values from -0.078125 to 0.078125
- down_weight: bfloat16 [8, 8192, 6144], P('dp', 'expert'), may hold values from -0.0625 to 0.0625
- shrinker: bfloat16 [8, 32, 6144], P('dp'), may hold values from -0.078125 to 0.078125
- widener: bfloat16 [8, 2, 16, 8192], P('dp', None, None, 'expert'), may hold values from -0.375 to 0.375
- squeezer: bfloat16 [8, 16, 8192], P('dp', None, 'expert'), may hold values from -0.0625 to 0.0625
- spreader: bfloat16 [8, 16, 6144], P('dp'), may hold values from -0.375 to 0.375
Outputs:
- token_grad: bfloat16 [2048, 6144], P('dp', 'expert')
- gate_grad: float32 [2048, 2], P('dp')
- shrinker_grad: float32 [8, 32, 6144], P('dp')
- widener_grad: float32 [8, 2, 16, 8192], P('dp', None, None, 'expert')
- squeezer_grad: float32 [8, 16, 8192], P('dp', None, 'expert')
- spreader_grad: float32 [8, 16, 6144], P('dp')
Inputs may be any that keep to these rules, and one draw needn't show every extreme that they name: `expert_choice`: each row names 2 different experts. Among the 256 tokens of one index of dp no expert is chosen more than 80 times, and some expert is chosen exactly 80 times by the tokens of some or all indices of dp.
All inputs are finite; a program needn't handle non-finite values.
Results may differ from a plain program's by a relative error of at most 0.02.
Values may be sent and summed in bfloat16 or wider, within the bound.
No kernel may reach another device: no remote copies, remote signals or barrier semaphores. Data moves between devices by JAX's collectives and lax.ppermute only.
A program may use at most 128 MiB of HBM per device.

v0:
```python
import jax
import jax.numpy as jnp
from jax import lax
from jax.sharding import PartitionSpec as P

adapter_scale = 2.0


def product(pattern, operand_a, operand_b):
    return jnp.einsum(pattern, operand_a, operand_b, preferred_element_type=jnp.float32)


def silu_pair(gate_pre):
    logistic = jax.nn.sigmoid(gate_pre)
    return (gate_pre * logistic, logistic * (1.0 + gate_pre * (1.0 - logistic)))


def full_rows(gathered, capacity, part_width):
    n_groups = gathered.shape[0]
    n_sources = gathered.shape[1]
    ordered = gathered.reshape(n_groups, n_sources, capacity, part_width).transpose(1, 2, 0, 3)
    return ordered.reshape(n_sources * capacity, n_groups * part_width)


def local(
    tokens,
    cotangent,
    expert_choice,
    gate_values,
    gate_weight,
    up_weight,
    down_weight,
    shrinker,
    widener,
    squeezer,
    spreader,
):
    tok_rows, part_width = tokens.shape
    top_k = expert_choice.shape[1]
    low_rank = spreader.shape[1]
    n_groups = lax.axis_size("expert")
    n_experts = lax.axis_size("dp")
    capacity = tok_rows * top_k * 5 // (4 * n_experts)
    own_rows = n_experts * capacity
    flat_choice = expert_choice.reshape(-1)
    onehot = (flat_choice[:, None] == jnp.arange(n_experts, dtype=jnp.int32)[None, :]).astype(
        jnp.int32
    )
    before = jnp.cumsum(onehot, axis=0) - onehot
    slot_index = jnp.sum(before * onehot, axis=1)
    target = flat_choice * capacity + slot_index
    placing = target[None, :] == jnp.arange(own_rows, dtype=jnp.int32)[:, None]
    stacked = jnp.repeat(jnp.concatenate([tokens, cotangent], axis=1), top_k, axis=0)
    placed = jnp.dot(
        placing.astype(jnp.bfloat16), stacked, preferred_element_type=jnp.float32
    ).astype(jnp.bfloat16)
    send_x = placed[:, :part_width].reshape(n_experts, capacity * part_width)
    send_dy = placed[:, part_width:].reshape(n_experts, capacity * part_width)
    gate_flat = gate_values.reshape(-1).astype(jnp.float32)
    send_gate = (
        jnp.sum(jnp.where(placing, gate_flat[None, :], 0.0), axis=1)
        .astype(jnp.bfloat16)
        .reshape(n_experts, capacity)
    )
    recv_x, recv_dy, recv_gate = (
        lax.all_to_all(send_x, "dp", split_axis=0, concat_axis=0, tiled=True),
        lax.all_to_all(send_dy, "dp", split_axis=0, concat_axis=0, tiled=True),
        lax.all_to_all(send_gate, "dp", split_axis=0, concat_axis=0, tiled=True),
    )
    gate_rows = recv_gate.reshape(-1).astype(jnp.float32)
    gathered_x, gathered_dy = (
        lax.all_gather(recv_x[None], "expert", axis=0, tiled=True),
        lax.all_gather(recv_dy[None], "expert", axis=0, tiled=True),
    )
    rows_dy = full_rows(gathered_dy, capacity, part_width)
    rows_x = full_rows(gathered_x, capacity, part_width)
    shrink_local = shrinker[0]
    widen_local = widener[0]
    squeeze_local = squeezer[0]
    spread_local = spreader[0]
    lowrank_in = product("nd,rd->nr", rows_x, shrink_local).astype(jnp.bfloat16)
    gate_pre = jnp.dot(
        rows_x, gate_weight[0], preferred_element_type=jnp.float32
    ) + adapter_scale * jnp.dot(
        lowrank_in[:, :low_rank], widen_local[0], preferred_element_type=jnp.float32
    )
    up_pre = jnp.dot(
        rows_x, up_weight[0], preferred_element_type=jnp.float32
    ) + adapter_scale * jnp.dot(
        lowrank_in[:, low_rank:], widen_local[1], preferred_element_type=jnp.float32
    )
    silu_gate, silu_slope = silu_pair(gate_pre)
    activation = (silu_gate * up_pre).astype(jnp.bfloat16)
    out_part = product("rf,nf->rn", squeeze_local, activation)
    out_low = lax.psum(out_part.astype(jnp.bfloat16), "expert").astype(jnp.float32)
    back_down = product("nd,fd->nf", rows_dy, down_weight[0])
    back_low = product("rd,nd->rn", spread_local, rows_dy)
    gate_part = jnp.sum(activation.astype(jnp.float32) * back_down, axis=1)
    scaled_low = (back_low * gate_rows[None, :]).astype(jnp.bfloat16)
    act_delta = gate_rows[:, None] * back_down + adapter_scale * product(
        "rn,rf->nf", scaled_low, squeeze_local
    )
    gate_delta = (act_delta * up_pre * silu_slope).astype(jnp.bfloat16)
    up_delta = (act_delta * silu_gate).astype(jnp.bfloat16)
    back_part = jnp.concatenate(
        [
            product("rf,nf->rn", widen_local[0], gate_delta),
            product("rf,nf->rn", widen_local[1], up_delta),
        ],
        axis=0,
    )
    back_sum, gate_sum = (
        lax.psum(back_part.astype(jnp.bfloat16), "expert").astype(jnp.float32),
        lax.psum(gate_part.astype(jnp.bfloat16), "expert").astype(jnp.float32),
    )
    low_out = out_low.astype(jnp.bfloat16)
    gate_dots = gate_sum + adapter_scale * jnp.sum(low_out.astype(jnp.float32) * back_low, axis=0)
    back_in = back_sum.astype(jnp.bfloat16)
    gate_blocks = gate_weight[0].reshape(n_groups, part_width, gate_weight.shape[2])
    up_blocks = up_weight[0].reshape(n_groups, part_width, up_weight.shape[2])
    term = product("nf,kdf->knd", gate_delta, gate_blocks) + product(
        "nf,kdf->knd", up_delta, up_blocks
    )
    token_part = (
        lax.psum_scatter(
            term.reshape(1 * lax.axis_size("expert"), own_rows * part_width).astype(jnp.bfloat16),
            "expert",
            scatter_dimension=0,
            tiled=True,
        )
        .astype(jnp.float32)
        .reshape(own_rows, part_width)
    )
    shrink_cols = lax.dynamic_slice_in_dim(
        shrink_local, lax.axis_index("expert") * part_width, part_width, 1
    )
    token_part = token_part + adapter_scale * product("rn,rd->nd", back_in, shrink_cols)
    token_back, gate_back = (
        lax.all_to_all(
            token_part.reshape(n_experts, capacity * part_width).astype(jnp.bfloat16),
            "dp",
            split_axis=0,
            concat_axis=0,
            tiled=True,
        ).astype(jnp.float32),
        lax.all_to_all(
            gate_dots.reshape(n_experts, capacity).astype(jnp.bfloat16),
            "dp",
            split_axis=0,
            concat_axis=0,
            tiled=True,
        ).astype(jnp.float32),
    )
    picked = jnp.take(token_back.reshape(own_rows, part_width), target, axis=0)
    token_grad = jnp.sum(picked.reshape(tok_rows, top_k, part_width), axis=1).astype(jnp.bfloat16)
    gate_grad = jnp.take(gate_back.reshape(own_rows), target).reshape(tok_rows, top_k)
    shrinker_grad = adapter_scale * product("rn,nd->rd", back_in, rows_x)
    widener_grad = adapter_scale * jnp.stack(
        [
            product("nr,nf->rf", lowrank_in[:, :low_rank], gate_delta),
            product("nr,nf->rf", lowrank_in[:, low_rank:], up_delta),
        ]
    )
    squeezer_grad = adapter_scale * product("rn,nf->rf", scaled_low, activation)
    weighted_low = (out_low * gate_rows[None, :]).astype(jnp.bfloat16)
    spreader_grad = adapter_scale * product("rn,nd->rd", weighted_low, rows_dy)
    return (
        token_grad,
        gate_grad,
        shrinker_grad[None],
        widener_grad[None],
        squeezer_grad[None],
        spreader_grad[None],
    )


def solution(mesh):
    placed = (
        P("dp", "expert"),
        P("dp", "expert"),
        P("dp", None),
        P("dp", None),
        P("dp", None, "expert"),
        P("dp", None, "expert"),
        P("dp", "expert", None),
        P("dp", None, None),
        P("dp", None, None, "expert"),
        P("dp", None, "expert"),
        P("dp", None, None),
    )
    return jax.shard_map(
        local,
        mesh=mesh,
        in_specs=placed,
        out_specs=(
            P("dp", "expert"),
            P("dp", None),
            P("dp", None, None),
            P("dp", None, None, "expert"),
            P("dp", None, "expert"),
            P("dp", None, None),
        ),
        check_vma=False,
    )
```

profile of v0, /device:TPU:1, one launch (start us, length us, event | category | flops | bytes accessed | tf_op | source)
XLA Modules:
  0.0 594.0 jit_solution(10980135344185267276)
XLA Ops:
  21.3 3.0 reduce.16
  25.2 12.8 %all_to_all.38 = bf16[8,2,7680]{2,1,0:T(2,128)(2,1)S(1)} all-to-all(bf16[8,2,7680]{2,1,0:T(2,128)(2,1)} %reshape.290), channel_id=1, replica_groups=mesh['dp'=8,'expert'=32] {'dp'}, dimensions={0} | all-to-all | bytes 491520 | tf_op jit(solution)/shard_map/all_to_all | solution.py:67
  44.8 3.0 reduce.17
  48.7 10.7 %all_to_all.39 = bf16[8,2,7680]{2,1,0:T(2,128)(2,1)S(1)} all-to-all(bf16[8,2,7680]{2,1,0:T(2,128)(2,1)} %reshape.288), channel_id=1, replica_groups=mesh['dp'=8,'expert'=32] {'dp'}, dimensions={0} | all-to-all | bytes 491520 | tf_op jit(solution)/shard_map/all_to_all | solution.py:66
  62.7 8.1 %all_to_all.40 = bf16[8,1,80]{2,1,0:T(2,128)(2,1)S(1)} all-to-all(bf16[8,1,80]{2,1,0:T(2,128)(2,1)S(1)} %convert_element_type.180), channel_id=1, replica_groups=mesh['dp'=8,'expert'=32] {'dp'}, dimensions={0} | all-to-all | bytes 2560 | tf_op jit(solution)/shard_map/all_to_all | solution.py:68
  70.9 65.3 %all-gather.5.cloned.1.call-done = bf16[256,1,15360]{2,0,1:T(8,128)(2,1)} async-done(((bf16[8,1,15360]{2,0,1:T(8,128)(2,1)}), bf16[256,1,15360]{2,0,1:T(8,128)(2,1)}) %all-gather.5.cloned.1.call-update) | async-done | bytes 7864336 | tf_op jit(solution)/shard_map/all_gather | solution.py:73
  136.2 18.1 %reshape.231 = bf16[32,8,80,192]{3,2,1,0:T(8,128)(2,1)} reshape(bf16[256,1,15360]{2,0,1:T(8,128)(2,1)} %all-gather.5.cloned.1.call-done) | data formatting | bytes 15728640 | tf_op jit(solution)/shard_map/reshape | solution.py:21
  154.3 13.9 %copy.93 = bf16[8,80,32,192]{3,2,1,0:T(8,128)(2,1)} copy(bf16[8,80,32,192]{3,1,0,2:T(8,128)(2,1)} %bitcast.103) | data formatting | bytes 15728640 | tf_op jit(solution)/shard_map/transpose | solution.py:21
  168.2 18.2 %reshape.232 = bf16[640,6144]{1,0:T(8,128)(2,1)} reshape(bf16[8,80,32,192]{3,2,1,0:T(8,128)(2,1)} %copy.93) | data formatting | bytes 15728640 | tf_op jit(solution)/shard_map/reshape | solution.py:22
  186.4 6.0 %convolution_bitcast_fusion = f32[16,640]{1,0:T(8,128)S(1)} fusion(bf16[640,6144]{1,0:T(8,128)(2,1)} %reshape.232, bf16[1,16,6144]{2,1,0:T(8,128)(2,1)S(1)} %copy-done.8), kind=kOutput, calls=%fused_computation.28 | convolution fusion | flops 125829120 | bytes 8101888 | tf_op jit(solution)/shard_map/rd,nd->rn/dot_general | solution.py:10
  192.4 5.4 fusion.7
  197.8 33.9 %all-gather.7.cloned.1.call-done = bf16[256,1,15360]{2,0,1:T(8,128)(2,1)} async-done(((bf16[8,1,15360]{2,0,1:T(8,128)(2,1)}), bf16[256,1,15360]{2,0,1:T(8,128)(2,1)}) %all-gather.7.cloned.1.call-update) | async-done | bytes 7864336 | tf_op jit(solution)/shard_map/all_gather | solution.py:72
  231.7 18.3 %reshape.233 = bf16[32,8,80,192]{3,2,1,0:T(8,128)(2,1)} reshape(bf16[256,1,15360]{2,0,1:T(8,128)(2,1)} %all-gather.7.cloned.1.call-done) | data formatting | bytes 15728640 | tf_op jit(solution)/shard_map/reshape | solution.py:21
  249.9 13.8 %copy.98 = bf16[8,80,32,192]{3,2,1,0:T(8,128)(2,1)} copy(bf16[8,80,32,192]{3,1,0,2:T(8,128)(2,1)} %bitcast.104) | data formatting | bytes 15728640 | tf_op jit(solution)/shard_map/transpose | solution.py:21
  263.8 18.5 %reshape.234 = bf16[640,6144]{1,0:T(8,128)(2,1)} reshape(bf16[8,80,32,192]{3,2,1,0:T(8,128)(2,1)} %copy.98) | data formatting | bytes 15728640 | tf_op jit(solution)/shard_map/reshape | solution.py:22
  282.3 5.8 convolution_convert_fusion
  291.1 2.9 fusion.5
  295.9 6.8 %fusion.25 = f32[640,32,192]{0,2,1:T(8,128)} fusion(bf16[32,192,256]{2,1,0:T(8,128)(2,1)S(1)} %bitcast.102, bf16[640,256]{0,1:T(8,128)(2,1)S(1)} %get-tuple-element.37), kind=kOutput, calls=%fused_computation.53 | convolution fusion | flops 2013265920 | bytes 19202048 | tf_op jit(solution)/shard_map/nf,kdf->knd/dot_general | solution.py:10
  302.7 8.8 %fusion.2 = bf16[32,640,192]{1,2,0:T(8,128)(2,1)} fusion(f32[640,32,192]{0,2,1:T(8,128)} %fusion.25, bf16[32,192,256]{2,1,0:T(8,128)(2,1)S(1)} %bitcast.105, bf16[640,256]{0,1:T(8,128)(2,1)S(1)} %get-tuple-element.38), kind=kOutput, calls=%fused_computation.7 | convolution fusion | flops 2021130240 | bytes 27066368 | tf_op jit(solution)/shard_map/nf,kdf->knd/dot_general | solution.py:10
  311.6 13.7 %copy.101 = bf16[32,640,192]{2,1,0:T(8,128)(2,1)} copy(bf16[32,640,192]{1,2,0:T(8,128)(2,1)} %fusion.2) | data formatting | bytes 15728640 | tf_op jit(solution)/shard_map/convert_element_type | solution.py:126
  325.3 15.6 %convert_element_type.158 = bf16[32,122880]{1,0:T(8,128)(2,1)} reshape(bf16[32,640,192]{2,1,0:T(8,128)(2,1)} %copy.101) | data formatting | bytes 15728640 | tf_op jit(solution)/shard_map/convert_element_type | solution.py:126
  345.9 114.8 %all-reduce.1 = (bf16[32,640]{1,0:T(8,128)(2,1)S(1)}, bf16[16,640]{1,0:T(8,128)(2,1)S(1)}, bf16[640]{0:T(1024)(128)(2,1)S(1)}) all-reduce(bf16[32,640]{1,0:T(8,128)(2,1)S(1)} %pad_maximum_fusion.1, bf16[16,640]{1,0:T(8,128)(2,1)S(1)} %fusion.18, bf16[640]{0:T(1024)(128)(2,1)S(1)} %get-tuple-element.35), channel_id=1, replica_groups=mesh['dp'=8,'expert'=32] {'expert'}, use_global_device_ids=true, to_apply=%region_5.6 | all-reduce | flops 31360 | bytes 125440 | tf_op jit(solution)/shard_map/psum | solution.py:113
  461.4 32.7 %all-to-all-start.4 = ((bf16[8,1,80]{2,1,0:T(2,128)(2,1)}), bf16[8,1,80]{2,1,0:T(2,128)(2,1)S(1)}, u32[]{:S(2)}, u32[]{:S(2)}) async-start(bf16[8,1,80]{2,1,0:T(2,128)(2,1)} %convert_element_type.182), calls=%async_computation.4 | async-start | bytes 8192 | tf_op jit(solution)/shard_map/all_to_all | solution.py:146
  498.3 5.3 fusion.1
  503.5 5.7 fusion
  513.0 30.8 %all-reduce.4.cloned.1.call-done = bf16[32,122880]{1,0:T(8,128)(2,1)} async-done(((bf16[32,122880]{1,0:T(8,128)(2,1)}), bf16[32,122880]{1,0:T(8,128)(2,1)}) %all-reduce.4.cloned.1.call-update) | async-done | bytes 7864336
  543.8 4.4 fusion.22
  556.8 3.0 reduce.18
  560.7 5.4 all-to-all-start.3
  569.4 3.0 all-to-all-done.3
  573.3 3.2 convert_reduce_fusion
  578.6 3.3 gather_fusion
  (106 shorter events, 65.4 us)
Async XLA Ops:
  7.2 280.9 %copy-start = (bf16[1,6144,256]{2,1,0:T(8,128)(2,1)S(1)}, bf16[1,6144,256]{2,1,0:T(8,128)(2,1)}, u32[]{:S(2)}) copy-start(bf16[1,6144,256]{2,1,0:T(8,128)(2,1)} %param.15) | copy-start | bytes 9437188
  7.2 54.9 %copy-start.12 = (bf16[256,2]{0,1:T(2,128)(2,1)S(1)}, bf16[256,2]{0,1:T(2,128)(2,1)}, u32[]{:S(2)}) copy-start(bf16[256,2]{0,1:T(2,128)(2,1)} %param.14) | copy-start | bytes 3076
  7.2 129.0 %all-gather.5.cloned.1.call-start = ((), (), s32[]{:S(2)}) async-start(), calls=%async_computation.5 | async-start | bytes 8110080 | tf_op jit(solution)/shard_map/all_gather | solution.py:73
  40.8 190.9 %all-gather.7.cloned.1.call-start = ((), (), s32[]{:S(2)}) async-start(), calls=%async_computation.6 | async-start | bytes 8110080 | tf_op jit(solution)/shard_map/all_gather | solution.py:72
  62.1 481.8 %all-reduce.4.cloned.1.call-start = ((), (), s32[]{:S(2)}) async-start(), calls=%async_computation.7 | async-start | bytes 15728640
  168.2 18.2 %copy-start.8 = (bf16[1,16,6144]{2,1,0:T(8,128)(2,1)S(1)}, bf16[1,16,6144]{2,1,0:T(8,128)(2,1)}, u32[]{:S(2)}) copy-start(bf16[1,16,6144]{2,1,0:T(8,128)(2,1)} %param.21) | copy-start | bytes 589828
  186.4 6.0 %copy-start.1 = (bf16[640,6144]{1,0:T(8,128)(2,1)S(1)}, bf16[640,6144]{1,0:T(8,128)(2,1)}, u32[]{:S(2)}) copy-start(bf16[640,6144]{1,0:T(8,128)(2,1)} %reshape.232) | copy-start | bytes 23592964
  282.3 5.8 copy-start.2
  288.1 2.9 copy-start.3
  291.0 3.0 copy-start.10
  291.0 3.3 copy-start.6
  291.0 3.3 copy-start.11
  295.9 6.8 %copy-start.5 = (bf16[640,256]{0,1:T(8,128)(2,1)}, bf16[640,256]{0,1:T(8,128)(2,1)S(1)}, u32[]{:S(2)}) copy-start(bf16[640,256]{0,1:T(8,128)(2,1)S(1)} %get-tuple-element.37) | copy-start | bytes 983044
  295.9 6.8 %copy-start.4 = (bf16[640,256]{0,1:T(8,128)(2,1)}, bf16[640,256]{0,1:T(8,128)(2,1)S(1)}, u32[]{:S(2)}) copy-start(bf16[640,256]{0,1:T(8,128)(2,1)S(1)} %get-tuple-element.38) | copy-start | bytes 983044
  340.8 1.0 copy-start.13
  460.7 48.6 %copy-start.7 = (bf16[32,640]{1,0:T(8,128)(2,1)}, bf16[32,640]{1,0:T(8,128)(2,1)S(1)}, u32[]{:S(2)}) copy-start(bf16[32,640]{1,0:T(8,128)(2,1)S(1)} %get-tuple-element.30) | copy-start | bytes 122884
  461.4 48.5 %all-to-all-start.4 = ((bf16[8,1,80]{2,1,0:T(2,128)(2,1)}), bf16[8,1,80]{2,1,0:T(2,128)(2,1)S(1)}, u32[]{:S(2)}, u32[]{:S(2)}) async-start(bf16[8,1,80]{2,1,0:T(2,128)(2,1)} %convert_element_type.182), calls=%async_computation.4 | async-start | bytes 8192 | tf_op jit(solution)/shard_map/all_to_all | solution.py:146
  560.7 11.7 %all-to-all-start.3 = ((bf16[8,2,7680]{2,1,0:T(2,128)(2,1)}), bf16[8,2,7680]{2,1,0:T(2,128)(2,1)S(1)}, u32[]{:S(2)}, u32[]{:S(2)}) async-start(bf16[8,2,7680]{2,1,0:T(2,128)(2,1)} %reshape.292), calls=%async_computation.3 | async-start | bytes 491520 | tf_op jit(solution)/shard_map/all_to_all | solution.py:139
  573.3 10.8 %copy-start.9 = (pred[256,2]{1,0:T(8,128)(4,1)S(1)}, pred[256,2]{1,0:T(8,128)(4,1)}, u32[]{:S(2)}) copy-start(pred[256,2]{1,0:T(8,128)(4,1)} %get-tuple-element.34) | copy-start | bytes 1540
Sparse Core Ops, SparseCore 0:
  40.9 95.2 all-gather.4
  139.3 92.2 all-gather.6
  341.0 202.8 all-reduce.3
where the time goes:
time: 603 us; the launch traced here: 594 us
  local copies, waits for them, and re-layouts  176 us (29%)
  blocking collectives  146 us (24%)
  waiting for transfers between devices  133 us (22%)
  matrix products  62 us (10%)
  starting transfers between devices  38.3 us (6%)
  other arithmetic  24 us (4%)
  between operations  14.3 us (2%)
    psum x1, blocking collectives, local(): lax.psum(back_part.astype(jnp.bfloat16), 'expert').astype(jnp.float32)  115 us
    all_gather x1, waiting for transfers between devices, local(): lax.all_gather(recv_dy[None], 'expert', axis=0, tiled=True)  65.3 us
    dot_general x15, matrix products, product(): jnp.einsum(pattern, operand_a, operand_b, preferred_element_type=jnp.floa...  53.1 us
    reshape x2, local copies, waits for them, and re-layouts, full_rows(): return ordered.reshape(n_sources * capacity, n_groups * part_width)  36.7 us
    reshape x2, local copies, waits for them, and re-layouts, full_rows(): gathered.reshape(n_groups, n_sources, capacity, part_width)  36.4 us
    all_gather x1, waiting for transfers between devices, local(): lax.all_gather(recv_x[None], 'expert', axis=0, tiled=True)  33.9 us
    all_to_all x1, starting transfers between devices, local(): lax.all_to_all(gate_dots.reshape(n_experts, capacity).astype(jnp.bfloat16...  32.7 us
    unnamed x4, waiting for transfers between devices  30.9 us
  transfers between devices with their start and end apart: 5, of which 4 were waited for; matrix products, arithmetic and copies ran while one was open for 17% of the time, Pallas kernels for 0%

commit v1 on v0

--- a/solution.py
+++ b/solution.py
@@ -70,7 +70,10 @@
     gate_rows = recv_gate.reshape(-1).astype(jnp.float32)
     gathered_x, gathered_dy = (
         lax.all_gather(recv_x[None], "expert", axis=0, tiled=True),
-        lax.all_gather(recv_dy[None], "expert", axis=0, tiled=True),
+        jnp.concatenate(
+            lax.all_to_all(jnp.stack([recv_dy[None]] * lax.axis_size("expert")), "expert", 0, 0),
+            axis=0,
+        ),
     )
     rows_dy = full_rows(gathered_dy, capacity, part_width)
     rows_x = full_rows(gathered_x, capacity, part_width)

time: 603 us -> 729 us (1.21)
  waiting for transfers between devices: 133 us -> 251 us
  blocking collectives: 146 us -> 118 us
  starting transfers between devices: 38.3 us -> 66.3 us
    all_to_all x0 -> x4, waiting for transfers between devices: none -> 216 us  [the longest x1 211 us: local(): lax.all_to_all(jnp.stack([recv_dy[None]] * lax.axis_size('expert')), 'exp...]
    all_gather x1 -> x0, waiting for transfers between devices: 65.3 us -> none  [local(): lax.all_gather(recv_dy[None], 'expert', axis=0, tiled=True)]
    all_gather x1, waiting for transfers between devices: 33.9 us -> 0.01 us  [local(): lax.all_gather(recv_x[None], 'expert', axis=0, tiled=True)]
    all_to_all x3 -> x0, blocking collectives: 31.6 us -> none  [the longest x1 12.8 us: local(): lax.all_to_all(send_dy, 'dp', split_axis=0, concat_axis=0, tiled=True)]
    all_to_all x0 -> x4, starting transfers between devices: none -> 26.7 us  [the longest x1 10.7 us: local(): lax.all_to_all(jnp.stack([recv_dy[None]] * lax.axis_size('expert')), 'exp...]
    another operation x1 -> x3, local copies, waits for them, and re-layouts: 0.01 us -> 22.1 us  [the longest x1 18.1 us: full_rows(): gathered.reshape(n_groups, n_sources, capacity, part_width)]
    reshape x2 -> x1, local copies, waits for them, and re-layouts: 36.4 us -> 18.3 us  [full_rows(): gathered.reshape(n_groups, n_sources, capacity, part_width)]
    unnamed x4 -> x3, waiting for transfers between devices: 30.9 us -> 32.3 us
  transfers between devices with their start and end apart: 5 -> 8, of which waited for: 4 -> 4; matrix products, arithmetic and copies ran while one was open for 17% -> 16% of each run, Pallas kernels for 0% -> 0%
where the time goes in v1:
time: 729 us; the launch traced here: 719 us
  waiting for transfers between devices  251 us (34%)
  local copies, waits for them, and re-layouts  182 us (25%)
  blocking collectives  118 us (16%)
  starting transfers between devices  66.3 us (9%)
  matrix products  61.5 us (8%)
  other arithmetic  24.7 us (3%)
  between operations  14.6 us (2%)
    all_to_all x1, waiting for transfers between devices, local(): lax.all_to_all(jnp.stack([recv_dy[None]] * lax.axis_size('expert')), 'exp...  211 us
    psum x1, blocking collectives, local(): lax.psum(back_part.astype(jnp.bfloat16), 'expert').astype(jnp.float32)  118 us
    dot_general x15, matrix products, product(): jnp.einsum(pattern, operand_a, operand_b, preferred_element_type=jnp.floa...  52.5 us
    reshape x2, local copies, waits for them, and re-layouts, full_rows(): return ordered.reshape(n_sources * capacity, n_groups * part_width)  36.7 us
    all_to_all x1, starting transfers between devices, local(): lax.all_to_all(gate_dots.reshape(n_experts, capacity).astype(jnp.bfloat16...  34 us
    unnamed x3, waiting for transfers between devices  32.3 us
    convert_element_type x2, local copies, waits for them, and re-layouts, local(): term.reshape(1 * lax.axis_size('expert'), own_rows * part_width)  29.3 us
    transpose x2, local copies, waits for them, and re-layouts, full_rows(): gathered.reshape(n_groups, n_sources, capacity, part_width)  27.7 us
  transfers between devices with their start and end apart: 8, of which 4 were waited for; matrix products, arithmetic and copies ran while one was open for 16% of the time, Pallas kernels for 0%

profile of v1, /device:TPU:1, one launch (start us, length us, event | category | flops | bytes accessed | tf_op | source)
XLA Modules:
  0.0 719.1 jit_solution(5065830964357112226)
XLA Ops:
  11.8 6.4 all-to-all-start
  29.5 3.0 reduce.16
  33.4 4.8 all-to-all-start.1
  42.2 3.7 reduce.17
  47.7 4.8 all-to-all-start.3
  54.5 4.4 all-to-all-done.3
  58.9 4.0 stack.12
  62.9 10.7 %all-to-all-start.2 = ((bf16[32,1,8,15360]{3,2,1,0:T(8,128)(2,1)}), bf16[32,1,8,15360]{3,2,1,0:T(8,128)(2,1)}, u32[]{:S(2)}, u32[]{:S(2)}) async-start(bf16[32,1,8,15360]{3,2,1,0:T(8,128)(2,1)} %stack.12), calls=%async_computation.2 | async-start | bytes 15728640 | tf_op jit(solution)/shard_map/all_to_all | solution.py:74
  77.6 211.4 %all-to-all-done.2 = bf16[32,1,8,15360]{3,2,1,0:T(8,128)(2,1)} async-done(((bf16[32,1,8,15360]{3,2,1,0:T(8,128)(2,1)}), bf16[32,1,8,15360]{3,2,1,0:T(8,128)(2,1)}, u32[]{:S(2)}, u32[]{:S(2)}) %all-to-all-start.2) | async-done | bytes 7864352 | tf_op jit(solution)/shard_map/all_to_all | solution.py:74
  289.1 18.1 %reshape_reshape.3 = bf16[32,8,80,192]{3,2,1,0:T(8,128)(2,1)} reshape(bf16[32,1,8,15360]{3,2,1,0:T(8,128)(2,1)} %all-to-all-done.2) | data formatting | bytes 15728640 | tf_op jit(solution)/shard_map/reshape;reshape | solution.py:21
  307.1 13.8 %copy.106 = bf16[8,80,32,192]{3,2,1,0:T(8,128)(2,1)} copy(bf16[8,80,32,192]{3,1,0,2:T(8,128)(2,1)} %bitcast.106) | data formatting | bytes 15728640 | tf_op jit(solution)/shard_map/transpose | solution.py:21
  321.0 18.1 %reshape.232 = bf16[640,6144]{1,0:T(8,128)(2,1)} reshape(bf16[8,80,32,192]{3,2,1,0:T(8,128)(2,1)} %copy.106) | data formatting | bytes 15728640 | tf_op jit(solution)/shard_map/reshape | solution.py:22
  339.1 5.5 convolution_bitcast_fusion
  344.7 5.4 fusion.7
  350.1 18.3 %reshape.233 = bf16[32,8,80,192]{3,2,1,0:T(8,128)(2,1)} reshape(bf16[256,1,15360]{2,0,1:T(8,128)(2,1)} %all-gather.3.cloned.1.call-done) | data formatting | bytes 15728640 | tf_op jit(solution)/shard_map/reshape | solution.py:21
  368.3 13.8 %copy.111 = bf16[8,80,32,192]{3,2,1,0:T(8,128)(2,1)} copy(bf16[8,80,32,192]{3,1,0,2:T(8,128)(2,1)} %bitcast.107) | data formatting | bytes 15728640 | tf_op jit(solution)/shard_map/transpose | solution.py:21
  382.2 18.5 %reshape.234 = bf16[640,6144]{1,0:T(8,128)(2,1)} reshape(bf16[8,80,32,192]{3,2,1,0:T(8,128)(2,1)} %copy.111) | data formatting | bytes 15728640 | tf_op jit(solution)/shard_map/reshape | solution.py:22
  400.7 5.8 convolution_convert_fusion
  414.3 6.8 fusion.25
  421.1 8.8 %fusion.2 = bf16[32,640,192]{1,2,0:T(8,128)(2,1)} fusion(f32[640,32,192]{0,2,1:T(8,128)} %fusion.25, bf16[32,192,256]{2,1,0:T(8,128)(2,1)S(1)} %bitcast.108, bf16[640,256]{0,1:T(8,128)(2,1)S(1)} %get-tuple-element.44), kind=kOutput, calls=%fused_computation.7 | convolution fusion | flops 2021130240 | bytes 27066368 | tf_op jit(solution)/shard_map/nf,kdf->knd/dot_general | solution.py:10
  430.0 13.7 %copy.114 = bf16[32,640,192]{2,1,0:T(8,128)(2,1)} copy(bf16[32,640,192]{1,2,0:T(8,128)(2,1)} %fusion.2) | data formatting | bytes 15728640 | tf_op jit(solution)/shard_map/convert_element_type | solution.py:129
  443.7 15.6 %convert_element_type.158 = bf16[32,122880]{1,0:T(8,128)(2,1)} reshape(bf16[32,640,192]{2,1,0:T(8,128)(2,1)} %copy.114) | data formatting | bytes 15728640 | tf_op jit(solution)/shard_map/convert_element_type | solution.py:129
  464.3 118.5 %all-reduce.1 = (bf16[32,640]{1,0:T(8,128)(2,1)S(1)}, bf16[16,640]{1,0:T(8,128)(2,1)S(1)}, bf16[640]{0:T(1024)(128)(2,1)S(1)}) all-reduce(bf16[32,640]{1,0:T(8,128)(2,1)S(1)} %pad_maximum_fusion.1, bf16[16,640]{1,0:T(8,128)(2,1)S(1)} %fusion.18, bf16[640]{0:T(1024)(128)(2,1)S(1)} %get-tuple-element.41), channel_id=1, replica_groups=mesh['dp'=8,'expert'=32] {'expert'}, use_global_device_ids=true, to_apply=%region_5.6 | all-reduce | flops 31360 | bytes 125440 | tf_op jit(solution)/shard_map/psum | solution.py:116
  583.5 34.0 %all-to-all-start.5 = ((bf16[8,1,80]{2,1,0:T(2,128)(2,1)}), bf16[8,1,80]{2,1,0:T(2,128)(2,1)S(1)}, u32[]{:S(2)}, u32[]{:S(2)}) async-start(bf16[8,1,80]{2,1,0:T(2,128)(2,1)} %convert_element_type.182), calls=%async_computation.5 | async-start | bytes 8192 | tf_op jit(solution)/shard_map/all_to_all | solution.py:149
  621.7 5.3 fusion.1
  626.9 5.7 fusion
  636.4 32.2 %all-reduce.4.cloned.1.call-done = bf16[32,122880]{1,0:T(8,128)(2,1)} async-done(((bf16[32,122880]{1,0:T(8,128)(2,1)}), bf16[32,122880]{1,0:T(8,128)(2,1)}) %all-reduce.4.cloned.1.call-update) | async-done | bytes 7864336
  668.7 4.4 fusion.22
  681.6 3.0 reduce.18
  685.5 5.3 all-to-all-start.4
  698.0 3.2 convert_reduce_fusion
  703.4 3.3 gather_fusion
  (107 shorter events, 73.9 us)
Async XLA Ops:
  7.2 399.4 %copy-start = (bf16[1,6144,256]{2,1,0:T(8,128)(2,1)S(1)}, bf16[1,6144,256]{2,1,0:T(8,128)(2,1)}, u32[]{:S(2)}) copy-start(bf16[1,6144,256]{2,1,0:T(8,128)(2,1)} %param.15) | copy-start | bytes 9437188
  11.8 21.6 %all-to-all-start = ((bf16[8,1,80]{2,1,0:T(2,128)(2,1)}), bf16[8,1,80]{2,1,0:T(2,128)(2,1)S(1)}, u32[]{:S(2)}, u32[]{:S(2)}) async-start(bf16[8,1,80]{2,1,0:T(2,128)(2,1)} %convert_element_type.180), calls=%async_computation | async-start | bytes 8192 | tf_op jit(solution)/shard_map/all_to_all | solution.py:68
  33.4 14.3 %all-to-all-start.1 = ((bf16[8,2,7680]{2,1,0:T(2,128)(2,1)}), bf16[8,2,7680]{2,1,0:T(2,128)(2,1)S(1)}, u32[]{:S(2)}, u32[]{:S(2)}) async-start(bf16[8,2,7680]{2,1,0:T(2,128)(2,1)} %reshape.288), calls=%async_computation.1 | async-start | bytes 491520 | tf_op jit(solution)/shard_map/all_to_all | solution.py:67
  47.7 11.2 %all-to-all-start.3 = ((bf16[8,2,7680]{2,1,0:T(2,128)(2,1)}), bf16[8,2,7680]{2,1,0:T(2,128)(2,1)}, u32[]{:S(2)}, u32[]{:S(2)}) async-start(bf16[8,2,7680]{2,1,0:T(2,128)(2,1)} %reshape.286), calls=%async_computation.3 | async-start | bytes 491520 | tf_op jit(solution)/shard_map/all_to_all | solution.py:66
  62.9 226.1 %all-to-all-start.2 = ((bf16[32,1,8,15360]{3,2,1,0:T(8,128)(2,1)}), bf16[32,1,8,15360]{3,2,1,0:T(8,128)(2,1)}, u32[]{:S(2)}, u32[]{:S(2)}) async-start(bf16[32,1,8,15360]{3,2,1,0:T(8,128)(2,1)} %stack.12), calls=%async_computation.2 | async-start | bytes 15728640 | tf_op jit(solution)/shard_map/all_to_all | solution.py:74
  73.6 276.4 %all-gather.3.cloned.1.call-start = ((), (), s32[]{:S(2)}) async-start(), calls=%async_computation.6 | async-start | bytes 8110080 | tf_op jit(solution)/shard_map/all_gather | solution.py:72
  77.3 591.4 %all-reduce.4.cloned.1.call-start = ((), (), s32[]{:S(2)}) async-start(), calls=%async_computation.7 | async-start | bytes 15728640
  321.0 18.2 %copy-start.8 = (bf16[1,16,6144]{2,1,0:T(8,128)(2,1)S(1)}, bf16[1,16,6144]{2,1,0:T(8,128)(2,1)}, u32[]{:S(2)}) copy-start(bf16[1,16,6144]{2,1,0:T(8,128)(2,1)} %param.21) | copy-start | bytes 589828
  339.1 5.5 copy-start.1
  400.7 5.8 copy-start.2
  406.5 2.9 copy-start.3
  409.4 3.0 copy-start.10
  409.4 3.3 copy-start.6
  409.4 3.3 copy-start.11
  414.3 6.8 copy-start.5
  414.3 6.8 copy-start.4
  459.2 1.0 copy-start.12
  582.7 49.9 %copy-start.7 = (bf16[32,640]{1,0:T(8,128)(2,1)}, bf16[32,640]{1,0:T(8,128)(2,1)S(1)}, u32[]{:S(2)}) copy-start(bf16[32,640]{1,0:T(8,128)(2,1)S(1)} %get-tuple-element.36) | copy-start | bytes 122884
  583.5 49.8 %all-to-all-start.5 = ((bf16[8,1,80]{2,1,0:T(2,128)(2,1)}), bf16[8,1,80]{2,1,0:T(2,128)(2,1)S(1)}, u32[]{:S(2)}, u32[]{:S(2)}) async-start(bf16[8,1,80]{2,1,0:T(2,128)(2,1)} %convert_element_type.182), calls=%async_computation.5 | async-start | bytes 8192 | tf_op jit(solution)/shard_map/all_to_all | solution.py:149
  685.5 11.6 %all-to-all-start.4 = ((bf16[8,2,7680]{2,1,0:T(2,128)(2,1)}), bf16[8,2,7680]{2,1,0:T(2,128)(2,1)S(1)}, u32[]{:S(2)}, u32[]{:S(2)}) async-start(bf16[8,2,7680]{2,1,0:T(2,128)(2,1)} %reshape.290), calls=%async_computation.4 | async-start | bytes 491520 | tf_op jit(solution)/shard_map/all_to_all | solution.py:142
  698.0 10.8 %copy-start.9 = (pred[256,2]{1,0:T(8,128)(4,1)S(1)}, pred[256,2]{1,0:T(8,128)(4,1)}, u32[]{:S(2)}) copy-start(pred[256,2]{1,0:T(8,128)(4,1)} %get-tuple-element.40) | copy-start | bytes 1540
Sparse Core Ops, SparseCore 0:
  77.6 206.5 all-gather.2
  459.4 209.2 all-reduce.3
